TPU v7x, 32 devices: a whole 2x2x4 slice. The times are simulated.
32 devices in a mesh: row: 8 (over z, y), col: 4 (over x, core).
Axes of the slice: x: 2, y: 2, z: 4, core: 2. Of those that a mesh axis runs over, the one named last changes fastest.
Arguments:
- matrix_tiles: bfloat16 [8, 4, 96, 256, 256], P('row', 'col'), may hold values from -0.078125 to 0.078125
- tile_rows: int32 [8, 4, 96], P('row', 'col'), may hold values from 0 to 7, as said below
- tile_cols: int32 [8, 4, 96], P('row', 'col'), may hold values from 0 to 15
- tile_count: int32 [8, 4], P('row', 'col'), may hold values from 24 to 96, as said below
- x_start: float32 [16384, 256], P(('col', 'row')), may hold values from -5 to 5
- y_start: float32 [16384, 256], P(('row', 'col')), may hold values from 0 to 1
- cost_vector: float32 [16384, 256], P(('col', 'row')), may hold values from -6 to 6
- right_side: float32 [16384, 256], P(('row', 'col')), may hold values from -6 to 6
- lower_bound: float32 [16384, 256], P(('col', 'row')), may hold values from -1.5 to -0.3
- upper_bound: float32 [16384, 256], P(('col', 'row')), may hold values from 0.3 to 1.5
- step_primal: float32 [256], replicated, may hold values from 0.2 to 0.45
- step_dual: float32 [256], replicated, may hold values from 0.2 to 0.45
Outputs:
- primal_out: float32 [16384, 256], P(('col', 'row'))
- dual_out: float32 [16384, 256], P(('row', 'col'))
Inputs may be any that keep to these rules, and one draw needn't show every extreme that they name: Within one grid cell the pairs (tile_rows, tile_cols) of its slots are all different. `tile_count`: some grid cell has 96 used slots in every draw; slots at or above a cell's count are not part of A.
All inputs are finite; a program needn't handle non-finite values.
Results may differ from a plain program's by a relative error of at most 0.001.
Values may be sent and summed in bfloat16 or wider, within the bound.
A program may use at most 128 MiB of HBM per device.

v0:
```python
import jax
import jax.numpy as jnp
from jax import lax
from jax.sharding import PartitionSpec as P

NR_DEV = 8
SLOT_BLOCK = 16
eps = 1e-06


def forward_part(my_tiles, my_rows, my_cols, slot_count, segment):
    edge = my_tiles.shape[-1]
    batch_width = segment.shape[-1]
    x_tiles = segment.reshape(-1, edge, batch_width)
    slot_ids = jnp.arange(SLOT_BLOCK, dtype=jnp.int32)

    def forward_block_step(block_index, running):
        first_slot = block_index * SLOT_BLOCK
        tile_block = lax.dynamic_slice_in_dim(my_tiles, first_slot, SLOT_BLOCK, 0)
        row_block = lax.dynamic_slice_in_dim(my_rows, first_slot, SLOT_BLOCK, 0)
        col_block = lax.dynamic_slice_in_dim(my_cols, first_slot, SLOT_BLOCK, 0)
        in_use = first_slot + slot_ids < slot_count
        pieces = jnp.take(x_tiles, col_block, axis=0)
        products = jnp.einsum(
            "sij,sjb->sib", tile_block, pieces, preferred_element_type=jnp.float32
        )
        products = jnp.where(in_use[:, None, None], products, jnp.zeros_like(products))
        return running.at[row_block].add(products)

    blocks = (slot_count + SLOT_BLOCK - 1) // SLOT_BLOCK
    begin = jnp.zeros((NR_DEV, edge, batch_width), jnp.float32)
    return lax.fori_loop(0, blocks, forward_block_step, begin).reshape(-1, batch_width)


def backward_part(my_tiles, my_rows, my_cols, slot_count, segment, col_tiles):
    edge = my_tiles.shape[-1]
    batch_width = segment.shape[-1]
    y_tiles = segment.reshape(-1, edge, batch_width)
    slot_ids = jnp.arange(SLOT_BLOCK, dtype=jnp.int32)

    def backward_block_step(block_index, running):
        first_slot = block_index * SLOT_BLOCK
        tile_block = lax.dynamic_slice_in_dim(my_tiles, first_slot, SLOT_BLOCK, 0)
        row_block = lax.dynamic_slice_in_dim(my_rows, first_slot, SLOT_BLOCK, 0)
        col_block = lax.dynamic_slice_in_dim(my_cols, first_slot, SLOT_BLOCK, 0)
        in_use = first_slot + slot_ids < slot_count
        pieces = jnp.take(y_tiles, row_block, axis=0)
        products = jnp.einsum(
            "sij,sib->sjb", tile_block, pieces, preferred_element_type=jnp.float32
        )
        products = jnp.where(in_use[:, None, None], products, jnp.zeros_like(products))
        return running.at[col_block].add(products)

    blocks = (slot_count + SLOT_BLOCK - 1) // SLOT_BLOCK
    begin = jnp.zeros((col_tiles, edge, batch_width), jnp.float32)
    return lax.fori_loop(0, blocks, backward_block_step, begin).reshape(-1, batch_width)


def body(
    matrix_tiles,
    tile_rows,
    tile_cols,
    tile_count,
    x_start,
    y_start,
    cost_vector,
    right_side,
    lower_bound,
    upper_bound,
    step_primal,
    step_dual,
):
    my_tiles = matrix_tiles[0, 0]
    my_rows = tile_rows[0, 0]
    my_cols = tile_cols[0, 0]
    slot_count = tile_count[0, 0]
    row_devices = lax.axis_size("row")
    col_devices = lax.axis_size("col")
    share = x_start.shape[0]
    edge = my_tiles.shape[-1]
    col_tiles = share * row_devices // edge
    total_cols = share * row_devices * col_devices
    total_rows = y_start.shape[0] * row_devices * col_devices

    def dual_rows(values):
        return lax.all_gather(values.astype(jnp.bfloat16), "col", axis=0, tiled=True)

    def row_sums(segment):
        return lax.psum_scatter(
            forward_part(my_tiles, my_rows, my_cols, slot_count, segment),
            "col",
            scatter_dimension=0,
            tiled=True,
        )

    x_base, cost_seg, lower_seg, upper_seg = (x_start, cost_vector, lower_bound, upper_bound)

    def column_sums(segment):
        partial_value = backward_part(my_tiles, my_rows, my_cols, slot_count, segment, col_tiles)
        return lax.psum_scatter(partial_value, "row", scatter_dimension=0, tiled=True)

    def spread(ahead):
        return lax.all_gather(ahead, "row", axis=0, tiled=True)

    grad_zero = column_sums(dual_rows(y_start))
    primal_one = jnp.clip(x_base - step_primal * (cost_seg - grad_zero), lower_seg, upper_seg)
    primal_diff = primal_one - x_base
    move_primal = jnp.sum(primal_diff * primal_diff, axis=0)
    image_one = row_sums(spread((2.0 * primal_one - x_base).astype(jnp.bfloat16)))
    dual_one = jnp.maximum(y_start + step_dual * (right_side - image_one), 0.0)
    dual_diff = dual_one - y_start
    move_dual = jnp.sum(dual_diff * dual_diff, axis=0)
    move_primal, move_dual = lax.psum((move_primal, move_dual), ("row", "col"))
    weight = jnp.sqrt((move_dual / total_rows + eps) / (move_primal / total_cols + eps))
    grad_one = column_sums(dual_rows(dual_one))
    primal_two = jnp.clip(
        primal_one - step_primal / weight * (cost_seg - grad_one), lower_seg, upper_seg
    )
    image_two = row_sums(spread((2.0 * primal_two - primal_one).astype(jnp.bfloat16)))
    dual_out = jnp.maximum(dual_one + step_dual * weight * (right_side - image_two), 0.0)
    return (primal_two, dual_out)


def solution(mesh):
    placed = (
        P("row", "col", None, None, None),
        P("row", "col", None),
        P("row", "col", None),
        P("row", "col"),
        P(("col", "row"), None),
        P(("row", "col"), None),
        P(("col", "row"), None),
        P(("row", "col"), None),
        P(("col", "row"), None),
        P(("col", "row"), None),
        P(),
        P(),
    )
    return jax.shard_map(
        body,
        mesh=mesh,
        in_specs=placed,
        out_specs=(P(("col", "row"), None), P(("row", "col"), None)),
        check_vma=False,
    )
```

profile of v0, /device:TPU:0, one launch (start us, length us, event | category | flops | bytes accessed | tf_op | source)
XLA Modules:
  0.0 772.5 jit_solution(1718431034138353426)
XLA Ops:
  9.7 16.6 %copy.14 = bf16[96,256,256]{1,2,0:T(8,128)(2,1)} copy(bf16[96,256,256]{2,1,0:T(8,128)(2,1)} %bitcast.19) | data formatting | bytes 25165824
  31.9 91.8 %while.44 = (s32[]{:T(128)}, f32[16,256,256]{2,1,0:T(8,128)}, s32[]{:T(128)}, s32[96]{0:T(128)S(1)}, s32[]{:T(128)}, /*index=5*/bf16[96,256,256]{1,2,0:T(8,128)(...) while((s32[]{:T(128)}, f32[16,256,256]{2,1,0:T(8,128)}, ...), condition=%wide.region_2.4_spmd.clone, body=%wide.region_0.3_spmd.clone.sunk | while | flops 540017856 | bytes 25170616 | solution.py:56
  37.8 9.5 %scatter_fusion = f32[16,256,256]{2,1,0:T(8,128)} fusion(f32[16,256,256]{2,1,0:T(8,128)} %get-tuple-element.615, s32[16]{0:T(128)S(1)} %compare_select_fusion.16, f32[16,256,256]{2,1,0:T(8,128)} %convolution_select_fusion.8), kind=kCustom, calls=%fused_computation.4.clone.clone.1 | custom fusion | flops 1048576 | bytes 12582976 | tf_op jit(solution)/shard_map/while/body/scatter-add | solution.py:52
  53.2 9.5 %scatter_fusion = f32[16,256,256]{2,1,0:T(8,128)} fusion(f32[16,256,256]{2,1,0:T(8,128)} %get-tuple-element.615, s32[16]{0:T(128)S(1)} %compare_select_fusion.16, f32[16,256,256]{2,1,0:T(8,128)} %convolution_select_fusion.8), kind=kCustom, calls=%fused_computation.4.clone.clone.1 | custom fusion | flops 1048576 | bytes 12582976 | tf_op jit(solution)/shard_map/while/body/scatter-add | solution.py:52
  68.5 9.5 %scatter_fusion = f32[16,256,256]{2,1,0:T(8,128)} fusion(f32[16,256,256]{2,1,0:T(8,128)} %get-tuple-element.615, s32[16]{0:T(128)S(1)} %compare_select_fusion.16, f32[16,256,256]{2,1,0:T(8,128)} %convolution_select_fusion.8), kind=kCustom, calls=%fused_computation.4.clone.clone.1 | custom fusion | flops 1048576 | bytes 12582976 | tf_op jit(solution)/shard_map/while/body/scatter-add | solution.py:52
  83.8 9.5 %scatter_fusion = f32[16,256,256]{2,1,0:T(8,128)} fusion(f32[16,256,256]{2,1,0:T(8,128)} %get-tuple-element.615, s32[16]{0:T(128)S(1)} %compare_select_fusion.16, f32[16,256,256]{2,1,0:T(8,128)} %convolution_select_fusion.8), kind=kCustom, calls=%fused_computation.4.clone.clone.1 | custom fusion | flops 1048576 | bytes 12582976 | tf_op jit(solution)/shard_map/while/body/scatter-add | solution.py:52
  99.2 9.3 %scatter_fusion = f32[16,256,256]{2,1,0:T(8,128)} fusion(f32[16,256,256]{2,1,0:T(8,128)} %get-tuple-element.615, s32[16]{0:T(128)S(1)} %compare_select_fusion.16, f32[16,256,256]{2,1,0:T(8,128)} %convolution_select_fusion.8), kind=kCustom, calls=%fused_computation.4.clone.clone.1 | custom fusion | flops 1048576 | bytes 12582976 | tf_op jit(solution)/shard_map/while/body/scatter-add | solution.py:52
  114.3 9.5 %scatter_fusion = f32[16,256,256]{2,1,0:T(8,128)} fusion(f32[16,256,256]{2,1,0:T(8,128)} %get-tuple-element.615, s32[16]{0:T(128)S(1)} %compare_select_fusion.16, f32[16,256,256]{2,1,0:T(8,128)} %convolution_select_fusion.8), kind=kCustom, calls=%fused_computation.4.clone.clone.1 | custom fusion | flops 1048576 | bytes 12582976 | tf_op jit(solution)/shard_map/while/body/scatter-add | solution.py:52
  123.8 86.9 %reduce-scatter.5.cloned.1.call-done = f32[512,256]{1,0:T(8,128)} async-done(((f32[4096,256]{1,0:T(8,128)}), f32[512,256]{1,0:T(8,128)}) %reduce-scatter.5.cloned.1.call-update) | async-done | bytes 524304 | tf_op jit(solution)/shard_map/reduce_scatter | solution.py:100
  213.6 48.8 %all-gather.7.cloned.1.call-done = bf16[4096,256]{1,0:T(8,128)(2,1)} async-done(((bf16[512,256]{1,0:T(8,128)(2,1)}), bf16[4096,256]{1,0:T(8,128)(2,1)}) %all-gather.7.cloned.1.call-update) | async-done | bytes 2097168 | tf_op jit(solution)/shard_map/all_gather | solution.py:103
  262.6 93.1 %while.45 = (s32[]{:T(128)}, f32[8,256,256]{2,1,0:T(8,128)S(1)}, s32[]{:T(128)}, s32[96]{0:T(128)S(1)}, s32[]{:T(128)}, /*index=5*/bf16[96,256,256]{2,1,0:T(8,12...) while((s32[]{:T(128)}, f32[8,256,256]{2,1,0:T(8,128)S(1)}, ...), condition=%wide.region_6.9_spmd.clone, body=%wide.region_4.8_spmd.clone.sunk | while | flops 540017856 | bytes 25170616 | solution.py:32
  266.9 5.0 convolution_select_fusion.9
  271.9 6.1 scatter_fusion.1
  282.4 5.0 convolution_select_fusion.9
  287.5 6.2 scatter_fusion.1
  298.0 4.9 convolution_select_fusion.9
  303.0 6.1 scatter_fusion.1
  318.5 6.2 scatter_fusion.1
  329.0 4.9 convolution_select_fusion.9
  334.0 6.1 scatter_fusion.1
  344.5 4.9 convolution_select_fusion.9
  349.5 6.2 scatter_fusion.1
  357.1 28.9 %reduce-scatter.7.cloned.1.call-done = f32[512,256]{1,0:T(8,128)} async-done(((f32[2048,256]{1,0:T(8,128)}), f32[512,256]{1,0:T(8,128)}) %reduce-scatter.7.cloned.1.call-update) | async-done | bytes 524304 | tf_op jit(solution)/shard_map/reduce_scatter | solution.py:89
  388.8 16.8 %all-gather.9.cloned.1.call-done = bf16[2048,256]{1,0:T(8,128)(2,1)} async-done(((bf16[512,256]{1,0:T(8,128)(2,1)}), bf16[2048,256]{1,0:T(8,128)(2,1)}) %all-gather.9.cloned.1.call-update) | async-done | bytes 1048592 | tf_op jit(solution)/shard_map/all_gather | solution.py:86
  408.0 91.8 %while.46 = (s32[]{:T(128)}, f32[16,256,256]{2,1,0:T(8,128)}, s32[]{:T(128)}, s32[96]{0:T(128)S(1)}, s32[]{:T(128)}, /*index=5*/bf16[96,256,256]{1,2,0:T(8,128)(...) while((s32[]{:T(128)}, f32[16,256,256]{2,1,0:T(8,128)}, ...), condition=%wide.region_14.17_spmd.clone, body=%wide.region_12.16_spmd.clone.sunk | while | flops 540017856 | bytes 25170616 | solution.py:56
  413.8 9.5 %scatter_fusion.2 = f32[16,256,256]{2,1,0:T(8,128)} fusion(f32[16,256,256]{2,1,0:T(8,128)} %get-tuple-element.687, s32[16]{0:T(128)S(1)} %compare_select_fusion.18, f32[16,256,256]{2,1,0:T(8,128)} %convolution_select_fusion.10), kind=kCustom, calls=%fused_computation.6.clone.clone.1 | custom fusion | flops 1048576 | bytes 12582976 | tf_op jit(solution)/shard_map/while/body/scatter-add | solution.py:52
  429.2 9.5 %scatter_fusion.2 = f32[16,256,256]{2,1,0:T(8,128)} fusion(f32[16,256,256]{2,1,0:T(8,128)} %get-tuple-element.687, s32[16]{0:T(128)S(1)} %compare_select_fusion.18, f32[16,256,256]{2,1,0:T(8,128)} %convolution_select_fusion.10), kind=kCustom, calls=%fused_computation.6.clone.clone.1 | custom fusion | flops 1048576 | bytes 12582976 | tf_op jit(solution)/shard_map/while/body/scatter-add | solution.py:52
  444.5 9.5 %scatter_fusion.2 = f32[16,256,256]{2,1,0:T(8,128)} fusion(f32[16,256,256]{2,1,0:T(8,128)} %get-tuple-element.687, s32[16]{0:T(128)S(1)} %compare_select_fusion.18, f32[16,256,256]{2,1,0:T(8,128)} %convolution_select_fusion.10), kind=kCustom, calls=%fused_computation.6.clone.clone.1 | custom fusion | flops 1048576 | bytes 12582976 | tf_op jit(solution)/shard_map/while/body/scatter-add | solution.py:52
  459.8 9.5 %scatter_fusion.2 = f32[16,256,256]{2,1,0:T(8,128)} fusion(f32[16,256,256]{2,1,0:T(8,128)} %get-tuple-element.687, s32[16]{0:T(128)S(1)} %compare_select_fusion.18, f32[16,256,256]{2,1,0:T(8,128)} %convolution_select_fusion.10), kind=kCustom, calls=%fused_computation.6.clone.clone.1 | custom fusion | flops 1048576 | bytes 12582976 | tf_op jit(solution)/shard_map/while/body/scatter-add | solution.py:52
  475.1 9.4 %scatter_fusion.2 = f32[16,256,256]{2,1,0:T(8,128)} fusion(f32[16,256,256]{2,1,0:T(8,128)} %get-tuple-element.687, s32[16]{0:T(128)S(1)} %compare_select_fusion.18, f32[16,256,256]{2,1,0:T(8,128)} %convolution_select_fusion.10), kind=kCustom, calls=%fused_computation.6.clone.clone.1 | custom fusion | flops 1048576 | bytes 12582976 | tf_op jit(solution)/shard_map/while/body/scatter-add | solution.py:52
  490.3 9.4 %scatter_fusion.2 = f32[16,256,256]{2,1,0:T(8,128)} fusion(f32[16,256,256]{2,1,0:T(8,128)} %get-tuple-element.687, s32[16]{0:T(128)S(1)} %compare_select_fusion.18, f32[16,256,256]{2,1,0:T(8,128)} %convolution_select_fusion.10), kind=kCustom, calls=%fused_computation.6.clone.clone.1 | custom fusion | flops 1048576 | bytes 12582976 | tf_op jit(solution)/shard_map/while/body/scatter-add | solution.py:52
  499.8 40.9 %all-reduce = (f32[256]{0:T(256)S(1)}, f32[256]{0:T(256)S(1)}) all-reduce(f32[256]{0:T(256)S(1)} %get-tuple-element.372, f32[256]{0:T(256)S(1)} %get-tuple-element.370), channel_id=1, replica_groups=mesh['row'=8,'col'=4] {'row','col'}, use_global_device_ids=true, to_apply=%region_11.14 | all-reduce | flops 512 | bytes 4096 | tf_op jit(solution)/shard_map/psum | solution.py:113
  540.8 47.3 %reduce-scatter.9.cloned.1.call-done = f32[512,256]{1,0:T(8,128)} async-done(((f32[4096,256]{1,0:T(8,128)}), f32[512,256]{1,0:T(8,128)}) %reduce-scatter.9.cloned.1.call-update) | async-done | bytes 524304 | tf_op jit(solution)/shard_map/reduce_scatter | solution.py:100
  590.2 49.3 %all-gather.11.cloned.1.call-done = bf16[4096,256]{1,0:T(8,128)(2,1)} async-done(((bf16[512,256]{1,0:T(8,128)(2,1)}), bf16[4096,256]{1,0:T(8,128)(2,1)}) %all-gather.11.cloned.1.call-update) | async-done | bytes 2097168 | tf_op jit(solution)/shard_map/all_gather | solution.py:103
  639.7 93.7 %while.47 = (s32[]{:T(128)}, f32[8,256,256]{2,1,0:T(8,128)S(1)}, s32[]{:T(128)}, s32[96]{0:T(128)S(1)}, s32[]{:T(128)}, /*index=5*/bf16[96,256,256]{2,1,0:T(8,12...) while((s32[]{:T(128)}, f32[8,256,256]{2,1,0:T(8,128)S(1)}, ...), condition=%wide.region_18.21_spmd.clone, body=%wide.region_16.20_spmd.clone.sunk | while | flops 540017856 | bytes 25170616 | solution.py:32
  644.1 4.9 convolution_select_fusion.11
  649.1 6.1 scatter_fusion.3
  659.7 5.0 convolution_select_fusion.11
  664.7 6.2 scatter_fusion.3
  675.4 4.9 convolution_select_fusion.11
  680.4 6.1 scatter_fusion.3
  691.0 5.0 convolution_select_fusion.11
  696.0 6.2 scatter_fusion.3
  706.6 4.9 convolution_select_fusion.11
  711.6 6.1 scatter_fusion.3
  722.2 5.0 convolution_select_fusion.11
  727.2 6.2 scatter_fusion.3
  734.8 28.9 %reduce-scatter.11.cloned.1.call-done = f32[512,256]{1,0:T(8,128)} async-done(((f32[2048,256]{1,0:T(8,128)}), f32[512,256]{1,0:T(8,128)}) %reduce-scatter.11.cloned.1.call-update) | async-done | bytes 524304 | tf_op jit(solution)/shard_map/reduce_scatter | solution.py:89
  (183 shorter events, 150.5 us)
Async XLA Ops:
  7.2 22.4 %all-gather.5.cloned.1.call-start = ((), (), s32[]{:S(2)}) async-start(), calls=%async_computation.4 | async-start | bytes 1310720 | tf_op jit(solution)/shard_map/all_gather | solution.py:86
  9.0 201.7 %reduce-scatter.5.cloned.1.call-start = ((), (), s32[]{:S(2)}) async-start(), calls=%async_computation.5 | async-start | bytes 4718592 | tf_op jit(solution)/shard_map/reduce_scatter | solution.py:100
  29.6 2.4 copy-start.2
  29.6 2.4 copy-start.18
  29.6 2.4 copy-start.19
  123.7 87.0 %copy-start.9 = (f32[512,256]{1,0:T(8,128)S(1)}, f32[512,256]{1,0:T(8,128)}, u32[]{:S(2)}) copy-start(f32[512,256]{1,0:T(8,128)} %param.33) | copy-start | bytes 1572868
  123.7 87.0 %copy-start.11 = (f32[512,256]{1,0:T(8,128)S(1)}, f32[512,256]{1,0:T(8,128)}, u32[]{:S(2)}) copy-start(f32[512,256]{1,0:T(8,128)} %param.32) | copy-start | bytes 1572868
  123.7 87.0 %copy-start.13 = (f32[512,256]{1,0:T(8,128)S(1)}, f32[512,256]{1,0:T(8,128)}, u32[]{:S(2)}) copy-start(f32[512,256]{1,0:T(8,128)} %param.30) | copy-start | bytes 1572868
  123.7 87.0 %copy-start.17 = (f32[512,256]{1,0:T(8,128)S(1)}, f32[512,256]{1,0:T(8,128)}, u32[]{:S(2)}) copy-start(f32[512,256]{1,0:T(8,128)} %param.28) | copy-start | bytes 1572868
  123.8 87.0 %copy-start.21 = (f32[256]{0:T(256)S(1)}, f32[256]{0:T(256)}, u32[]{:S(2)}) copy-start(f32[256]{0:T(256)} %param.34) | copy-start | bytes 3076
  123.8 138.6 %all-gather.7.cloned.1.call-start = ((), (), s32[]{:S(2)}) async-start(), calls=%async_computation.6 | async-start | bytes 2359296 | tf_op jit(solution)/shard_map/all_gather | solution.py:103
  211.9 0.8 copy-start.6
  213.5 172.5 %reduce-scatter.7.cloned.1.call-start = ((), (), s32[]{:S(2)}) async-start(), calls=%async_computation.7 | async-start | bytes 2621440 | tf_op jit(solution)/shard_map/reduce_scatter | solution.py:89
  355.7 1.3 copy-start.1
  355.7 30.3 %copy-start.8 = (f32[512,256]{1,0:T(8,128)S(1)}, f32[512,256]{1,0:T(8,128)}, u32[]{:S(2)}) copy-start(f32[512,256]{1,0:T(8,128)} %param.29) | copy-start | bytes 1572868
  355.7 30.2 %copy-start.15 = (f32[512,256]{1,0:T(8,128)S(1)}, f32[512,256]{1,0:T(8,128)}, u32[]{:S(2)}) copy-start(f32[512,256]{1,0:T(8,128)} %param.31) | copy-start | bytes 1572868
  355.8 30.2 %copy-start.20 = (f32[256]{0:T(256)S(1)}, f32[256]{0:T(256)}, u32[]{:S(2)}) copy-start(f32[256]{0:T(256)} %param.35) | copy-start | bytes 3076
  357.1 48.6 %all-gather.9.cloned.1.call-start = ((), (), s32[]{:S(2)}) async-start(), calls=%async_computation.8 | async-start | bytes 1310720 | tf_op jit(solution)/shard_map/all_gather | solution.py:86
  387.2 0.8 copy-start.4
  388.7 199.3 %reduce-scatter.9.cloned.1.call-start = ((), (), s32[]{:S(2)}) async-start(), calls=%async_computation.9 | async-start | bytes 4718592 | tf_op jit(solution)/shard_map/reduce_scatter | solution.py:100
  405.6 2.4 copy-start.3
  499.8 88.3 %copy-start.7 = (f32[512,256]{1,0:T(8,128)S(1)}, f32[512,256]{1,0:T(8,128)}, u32[]{:S(2)}) copy-start(f32[512,256]{1,0:T(8,128)} %copy-done.6) | copy-start | bytes 1572868
  499.8 88.3 %copy-start.10 = (f32[512,256]{1,0:T(8,128)S(1)}, f32[512,256]{1,0:T(8,128)}, u32[]{:S(2)}) copy-start(f32[512,256]{1,0:T(8,128)} %param.33) | copy-start | bytes 1572868
  499.8 88.3 %copy-start.12 = (f32[512,256]{1,0:T(8,128)S(1)}, f32[512,256]{1,0:T(8,128)}, u32[]{:S(2)}) copy-start(f32[512,256]{1,0:T(8,128)} %param.32) | copy-start | bytes 1572868
  499.8 88.3 %copy-start.14 = (f32[512,256]{1,0:T(8,128)S(1)}, f32[512,256]{1,0:T(8,128)}, u32[]{:S(2)}) copy-start(f32[512,256]{1,0:T(8,128)} %param.30) | copy-start | bytes 1572868
  499.8 139.7 %all-gather.11.cloned.1.call-start = ((), (), s32[]{:S(2)}) async-start(), calls=%async_computation.10 | async-start | bytes 2359296 | tf_op jit(solution)/shard_map/all_gather | solution.py:103
  590.2 173.5 %reduce-scatter.11.cloned.1.call-start = ((), (), s32[]{:S(2)}) async-start(), calls=%async_computation.11 | async-start | bytes 2621440 | tf_op jit(solution)/shard_map/reduce_scatter | solution.py:89
  733.4 1.3 copy-start
  733.4 30.3 %copy-start.5 = (f32[512,256]{1,0:T(8,128)S(1)}, f32[512,256]{1,0:T(8,128)}, u32[]{:S(2)}) copy-start(f32[512,256]{1,0:T(8,128)} %copy-done.4) | copy-start | bytes 1572868
  733.4 30.3 %copy-start.16 = (f32[512,256]{1,0:T(8,128)S(1)}, f32[512,256]{1,0:T(8,128)}, u32[]{:S(2)}) copy-start(f32[512,256]{1,0:T(8,128)} %param.31) | copy-start | bytes 1572868
Sparse Core Ops, SparseCore 0:
  10.1 19.4 all-gather.4
  123.9 86.7 reduce-scatter.4
  213.6 48.7 all-gather.6
  357.2 28.7 reduce-scatter.6
  388.9 16.7 all-gather.8
  499.9 88.0 reduce-scatter.8
  590.8 48.7 all-gather.10
  734.9 28.7 reduce-scatter.10
where the time goes:
time: 775 us; the launch traced here: 772 us
  waiting for transfers between devices  310 us (40%)
  other arithmetic  217 us (28%)
  matrix products  111 us (14%)
  local copies, waits for them, and re-layouts  77.6 us (10%)
  blocking collectives  40.9 us (5%)
  between operations  15 us (2%)
    reduce_scatter x2, waiting for transfers between devices, column_sums(): lax.psum_scatter(partial_value, 'row', scatter_dimension=0, tiled=True)  134 us
    scatter-add x12, other arithmetic, backward_block_step(): return running.at[col_block].add(products)  114 us
    all_gather x2, waiting for transfers between devices, spread(): return lax.all_gather(ahead, 'row', axis=0, tiled=True)  98.1 us
    scatter-add x12, other arithmetic, forward_block_step(): return running.at[row_block].add(products)  73.9 us
    dot_general x12, matrix products, forward_block_step(): jnp.einsum('sij,sjb->sib', tile_block, pieces, preferred_element_type=jnp...  59.4 us
    reduce_scatter x2, waiting for transfers between devices, row_sums(): lax.psum_scatter(forward_part(my_tiles, my_rows, my_cols, slot_count, seg...  57.8 us
    dot_general x12, matrix products, backward_block_step(): jnp.einsum('sij,sib->sjb', tile_block, pieces, preferred_element_type=jnp...  51.9 us
    gather x12, local copies, waits for them, and re-layouts, forward_block_step(): pieces = jnp.take(x_tiles, col_block, axis=0)  43.4 us
  transfers between devices with their start and end apart: 8, of which 8 were waited for; matrix products, arithmetic and copies ran while one was open for 2% of the time, Pallas kernels for 0%

commit v1 on v0

--- a/solution.py
+++ b/solution.py
@@ -110,7 +110,7 @@
     dual_one = jnp.maximum(y_start + step_dual * (right_side - image_one), 0.0)
     dual_diff = dual_one - y_start
     move_dual = jnp.sum(dual_diff * dual_diff, axis=0)
-    move_primal, move_dual = lax.psum((move_primal, move_dual), ("row", "col"))
+    move_primal, move_dual = lax.psum(lax.psum((move_primal, move_dual), "row"), "col")
     weight = jnp.sqrt((move_dual / total_rows + eps) / (move_primal / total_cols + eps))
     grad_one = column_sums(dual_rows(dual_one))
     primal_two = jnp.clip(

time: 775 us -> 774 us (level)
  blocking collectives: 40.9 us -> 23.9 us
  waiting for transfers between devices: 310 us -> 326 us
    psum x1 -> x2, blocking collectives: 40.9 us -> 23.9 us  [the longest x1 17.8 us: body(): lax.psum((move_primal, move_dual), 'row')]
    reduce_scatter x2, waiting for transfers between devices: 134 us -> 150 us  [column_sums(): lax.psum_scatter(partial_value, 'row', scatter_dimension=0, tiled=True)]
where the time goes in v1:
time: 774 us; the launch traced here: 771 us
  waiting for transfers between devices  326 us (42%)
  other arithmetic  217 us (28%)
  matrix products  112 us (14%)
  local copies, waits for them, and re-layouts  77.5 us (10%)
  blocking collectives  23.9 us (3%)
  between operations  14.9 us (2%)
    reduce_scatter x2, waiting for transfers between devices, column_sums(): lax.psum_scatter(partial_value, 'row', scatter_dimension=0, tiled=True)  150 us
    scatter-add x12, other arithmetic, backward_block_step(): return running.at[col_block].add(products)  114 us
    all_gather x2, waiting for transfers between devices, spread(): return lax.all_gather(ahead, 'row', axis=0, tiled=True)  98.1 us
    scatter-add x12, other arithmetic, forward_block_step(): return running.at[row_block].add(products)  73.9 us
    dot_general x12, matrix products, forward_block_step(): jnp.einsum('sij,sjb->sib', tile_block, pieces, preferred_element_type=jnp...  59.5 us
    reduce_scatter x2, waiting for transfers between devices, row_sums(): lax.psum_scatter(forward_part(my_tiles, my_rows, my_cols, slot_count, seg...  57.8 us
    dot_general x12, matrix products, backward_block_step(): jnp.einsum('sij,sib->sjb', tile_block, pieces, preferred_element_type=jnp...  52 us
    gather x12, local copies, waits for them, and re-layouts, forward_block_step(): pieces = jnp.take(x_tiles, col_block, axis=0)  43.3 us
  transfers between devices with their start and end apart: 8, of which 8 were waited for; matrix products, arithmetic and copies ran while one was open for 2% of the time, Pallas kernels for 0%

profile of v1, /device:TPU:0, one launch (start us, length us, event | category | flops | bytes accessed | tf_op | source)
XLA Modules:
  0.0 771.5 jit_solution(18286484827768753943)
XLA Ops:
  9.7 16.6 %copy.14 = bf16[96,256,256]{1,2,0:T(8,128)(2,1)} copy(bf16[96,256,256]{2,1,0:T(8,128)(2,1)} %bitcast.19) | data formatting | bytes 25165824
  32.0 91.7 %while.44 = (s32[]{:T(128)}, f32[16,256,256]{2,1,0:T(8,128)}, s32[]{:T(128)}, s32[96]{0:T(128)S(1)}, s32[]{:T(128)}, /*index=5*/bf16[96,256,256]{1,2,0:T(8,128)(...) while((s32[]{:T(128)}, f32[16,256,256]{2,1,0:T(8,128)}, ...), condition=%wide.region_2.4_spmd.clone, body=%wide.region_0.3_spmd.clone.sunk | while | flops 540017856 | bytes 25170616 | solution.py:56
  37.8 9.5 %scatter_fusion = f32[16,256,256]{2,1,0:T(8,128)} fusion(f32[16,256,256]{2,1,0:T(8,128)} %get-tuple-element.617, s32[16]{0:T(128)S(1)} %compare_select_fusion.16, f32[16,256,256]{2,1,0:T(8,128)} %convolution_select_fusion.8), kind=kCustom, calls=%fused_computation.4.clone.clone.1 | custom fusion | flops 1048576 | bytes 12582976 | tf_op jit(solution)/shard_map/while/body/scatter-add | solution.py:52
  53.2 9.5 %scatter_fusion = f32[16,256,256]{2,1,0:T(8,128)} fusion(f32[16,256,256]{2,1,0:T(8,128)} %get-tuple-element.617, s32[16]{0:T(128)S(1)} %compare_select_fusion.16, f32[16,256,256]{2,1,0:T(8,128)} %convolution_select_fusion.8), kind=kCustom, calls=%fused_computation.4.clone.clone.1 | custom fusion | flops 1048576 | bytes 12582976 | tf_op jit(solution)/shard_map/while/body/scatter-add | solution.py:52
  68.5 9.5 %scatter_fusion = f32[16,256,256]{2,1,0:T(8,128)} fusion(f32[16,256,256]{2,1,0:T(8,128)} %get-tuple-element.617, s32[16]{0:T(128)S(1)} %compare_select_fusion.16, f32[16,256,256]{2,1,0:T(8,128)} %convolution_select_fusion.8), kind=kCustom, calls=%fused_computation.4.clone.clone.1 | custom fusion | flops 1048576 | bytes 12582976 | tf_op jit(solution)/shard_map/while/body/scatter-add | solution.py:52
  83.8 9.5 %scatter_fusion = f32[16,256,256]{2,1,0:T(8,128)} fusion(f32[16,256,256]{2,1,0:T(8,128)} %get-tuple-element.617, s32[16]{0:T(128)S(1)} %compare_select_fusion.16, f32[16,256,256]{2,1,0:T(8,128)} %convolution_select_fusion.8), kind=kCustom, calls=%fused_computation.4.clone.clone.1 | custom fusion | flops 1048576 | bytes 12582976 | tf_op jit(solution)/shard_map/while/body/scatter-add | solution.py:52
  99.1 9.3 %scatter_fusion = f32[16,256,256]{2,1,0:T(8,128)} fusion(f32[16,256,256]{2,1,0:T(8,128)} %get-tuple-element.617, s32[16]{0:T(128)S(1)} %compare_select_fusion.16, f32[16,256,256]{2,1,0:T(8,128)} %convolution_select_fusion.8), kind=kCustom, calls=%fused_computation.4.clone.clone.1 | custom fusion | flops 1048576 | bytes 12582976 | tf_op jit(solution)/shard_map/while/body/scatter-add | solution.py:52
  114.3 9.4 %scatter_fusion = f32[16,256,256]{2,1,0:T(8,128)} fusion(f32[16,256,256]{2,1,0:T(8,128)} %get-tuple-element.617, s32[16]{0:T(128)S(1)} %compare_select_fusion.16, f32[16,256,256]{2,1,0:T(8,128)} %convolution_select_fusion.8), kind=kCustom, calls=%fused_computation.4.clone.clone.1 | custom fusion | flops 1048576 | bytes 12582976 | tf_op jit(solution)/shard_map/while/body/scatter-add | solution.py:52
  123.8 87.0 %reduce-scatter.5.cloned.1.call-done = f32[512,256]{1,0:T(8,128)} async-done(((f32[4096,256]{1,0:T(8,128)}), f32[512,256]{1,0:T(8,128)}) %reduce-scatter.5.cloned.1.call-update) | async-done | bytes 524304 | tf_op jit(solution)/shard_map/reduce_scatter | solution.py:100
  213.6 48.8 %all-gather.7.cloned.1.call-done = bf16[4096,256]{1,0:T(8,128)(2,1)} async-done(((bf16[512,256]{1,0:T(8,128)(2,1)}), bf16[4096,256]{1,0:T(8,128)(2,1)}) %all-gather.7.cloned.1.call-update) | async-done | bytes 2097168 | tf_op jit(solution)/shard_map/all_gather | solution.py:103
  262.6 93.3 %while.45 = (s32[]{:T(128)}, f32[8,256,256]{2,1,0:T(8,128)S(1)}, s32[]{:T(128)}, s32[96]{0:T(128)S(1)}, s32[]{:T(128)}, /*index=5*/bf16[96,256,256]{2,1,0:T(8,12...) while((s32[]{:T(128)}, f32[8,256,256]{2,1,0:T(8,128)S(1)}, ...), condition=%wide.region_6.9_spmd.clone, body=%wide.region_4.8_spmd.clone.sunk | while | flops 540017856 | bytes 25170616 | solution.py:32
  267.0 5.0 convolution_select_fusion.9
  272.0 6.1 scatter_fusion.1
  282.5 5.0 convolution_select_fusion.9
  287.5 6.2 scatter_fusion.1
  303.1 6.1 scatter_fusion.1
  318.6 6.2 scatter_fusion.1
  329.2 5.0 convolution_select_fusion.9
  334.2 6.1 scatter_fusion.1
  344.7 5.0 convolution_select_fusion.9
  349.7 6.2 scatter_fusion.1
  357.3 28.9 %reduce-scatter.7.cloned.1.call-done = f32[512,256]{1,0:T(8,128)} async-done(((f32[2048,256]{1,0:T(8,128)}), f32[512,256]{1,0:T(8,128)}) %reduce-scatter.7.cloned.1.call-update) | async-done | bytes 524304 | tf_op jit(solution)/shard_map/reduce_scatter | solution.py:89
  389.0 16.8 %all-gather.9.cloned.1.call-done = bf16[2048,256]{1,0:T(8,128)(2,1)} async-done(((bf16[512,256]{1,0:T(8,128)(2,1)}), bf16[2048,256]{1,0:T(8,128)(2,1)}) %all-gather.9.cloned.1.call-update) | async-done | bytes 1048592 | tf_op jit(solution)/shard_map/all_gather | solution.py:86
  408.2 91.9 %while.46 = (s32[]{:T(128)}, f32[16,256,256]{2,1,0:T(8,128)}, s32[]{:T(128)}, s32[96]{0:T(128)S(1)}, s32[]{:T(128)}, /*index=5*/bf16[96,256,256]{1,2,0:T(8,128)(...) while((s32[]{:T(128)}, f32[16,256,256]{2,1,0:T(8,128)}, ...), condition=%wide.region_16.19_spmd.clone, body=%wide.region_14.18_spmd.clone.sunk | while | flops 540017856 | bytes 25170616 | solution.py:56
  414.0 9.5 %scatter_fusion.2 = f32[16,256,256]{2,1,0:T(8,128)} fusion(f32[16,256,256]{2,1,0:T(8,128)} %get-tuple-element.689, s32[16]{0:T(128)S(1)} %compare_select_fusion.18, f32[16,256,256]{2,1,0:T(8,128)} %convolution_select_fusion.10), kind=kCustom, calls=%fused_computation.6.clone.clone.1 | custom fusion | flops 1048576 | bytes 12582976 | tf_op jit(solution)/shard_map/while/body/scatter-add | solution.py:52
  429.3 9.6 %scatter_fusion.2 = f32[16,256,256]{2,1,0:T(8,128)} fusion(f32[16,256,256]{2,1,0:T(8,128)} %get-tuple-element.689, s32[16]{0:T(128)S(1)} %compare_select_fusion.18, f32[16,256,256]{2,1,0:T(8,128)} %convolution_select_fusion.10), kind=kCustom, calls=%fused_computation.6.clone.clone.1 | custom fusion | flops 1048576 | bytes 12582976 | tf_op jit(solution)/shard_map/while/body/scatter-add | solution.py:52
  444.8 9.5 %scatter_fusion.2 = f32[16,256,256]{2,1,0:T(8,128)} fusion(f32[16,256,256]{2,1,0:T(8,128)} %get-tuple-element.689, s32[16]{0:T(128)S(1)} %compare_select_fusion.18, f32[16,256,256]{2,1,0:T(8,128)} %convolution_select_fusion.10), kind=kCustom, calls=%fused_computation.6.clone.clone.1 | custom fusion | flops 1048576 | bytes 12582976 | tf_op jit(solution)/shard_map/while/body/scatter-add | solution.py:52
  460.1 9.4 %scatter_fusion.2 = f32[16,256,256]{2,1,0:T(8,128)} fusion(f32[16,256,256]{2,1,0:T(8,128)} %get-tuple-element.689, s32[16]{0:T(128)S(1)} %compare_select_fusion.18, f32[16,256,256]{2,1,0:T(8,128)} %convolution_select_fusion.10), kind=kCustom, calls=%fused_computation.6.clone.clone.1 | custom fusion | flops 1048576 | bytes 12582976 | tf_op jit(solution)/shard_map/while/body/scatter-add | solution.py:52
  475.4 9.4 %scatter_fusion.2 = f32[16,256,256]{2,1,0:T(8,128)} fusion(f32[16,256,256]{2,1,0:T(8,128)} %get-tuple-element.689, s32[16]{0:T(128)S(1)} %compare_select_fusion.18, f32[16,256,256]{2,1,0:T(8,128)} %convolution_select_fusion.10), kind=kCustom, calls=%fused_computation.6.clone.clone.1 | custom fusion | flops 1048576 | bytes 12582976 | tf_op jit(solution)/shard_map/while/body/scatter-add | solution.py:52
  490.6 9.5 %scatter_fusion.2 = f32[16,256,256]{2,1,0:T(8,128)} fusion(f32[16,256,256]{2,1,0:T(8,128)} %get-tuple-element.689, s32[16]{0:T(128)S(1)} %compare_select_fusion.18, f32[16,256,256]{2,1,0:T(8,128)} %convolution_select_fusion.10), kind=kCustom, calls=%fused_computation.6.clone.clone.1 | custom fusion | flops 1048576 | bytes 12582976 | tf_op jit(solution)/shard_map/while/body/scatter-add | solution.py:52
  500.2 17.8 %all-reduce = (f32[256]{0:T(256)S(1)}, f32[256]{0:T(256)S(1)}) all-reduce(f32[256]{0:T(256)S(1)} %get-tuple-element.374, f32[256]{0:T(256)S(1)} %get-tuple-element.372), channel_id=1, replica_groups=mesh['row'=8,'col'=4] {'row'}, use_global_device_ids=true, to_apply=%region_12.15 | all-reduce | flops 512 | bytes 4096 | tf_op jit(solution)/shard_map/psum | solution.py:113
  518.0 6.0 all-reduce.1
  524.1 63.0 %reduce-scatter.9.cloned.1.call-done = f32[512,256]{1,0:T(8,128)} async-done(((f32[4096,256]{1,0:T(8,128)}), f32[512,256]{1,0:T(8,128)}) %reduce-scatter.9.cloned.1.call-update) | async-done | bytes 524304 | tf_op jit(solution)/shard_map/reduce_scatter | solution.py:100
  589.3 49.3 %all-gather.11.cloned.1.call-done = bf16[4096,256]{1,0:T(8,128)(2,1)} async-done(((bf16[512,256]{1,0:T(8,128)(2,1)}), bf16[4096,256]{1,0:T(8,128)(2,1)}) %all-gather.11.cloned.1.call-update) | async-done | bytes 2097168 | tf_op jit(solution)/shard_map/all_gather | solution.py:103
  638.7 93.6 %while.47 = (s32[]{:T(128)}, f32[8,256,256]{2,1,0:T(8,128)S(1)}, s32[]{:T(128)}, s32[96]{0:T(128)S(1)}, s32[]{:T(128)}, /*index=5*/bf16[96,256,256]{2,1,0:T(8,12...) while((s32[]{:T(128)}, f32[8,256,256]{2,1,0:T(8,128)S(1)}, ...), condition=%wide.region_20.23_spmd.clone, body=%wide.region_18.22_spmd.clone.sunk | while | flops 540017856 | bytes 25170616 | solution.py:32
  643.1 5.0 convolution_select_fusion.11
  648.2 6.1 scatter_fusion.3
  658.7 5.0 convolution_select_fusion.11
  663.8 6.2 scatter_fusion.3
  674.4 5.0 convolution_select_fusion.11
  679.4 6.1 scatter_fusion.3
  690.0 5.0 convolution_select_fusion.11
  695.0 6.2 scatter_fusion.3
  705.6 5.0 convolution_select_fusion.11
  710.6 6.1 scatter_fusion.3
  721.2 5.0 convolution_select_fusion.11
  726.2 6.2 scatter_fusion.3
  733.7 28.9 %reduce-scatter.11.cloned.1.call-done = f32[512,256]{1,0:T(8,128)} async-done(((f32[2048,256]{1,0:T(8,128)}), f32[512,256]{1,0:T(8,128)}) %reduce-scatter.11.cloned.1.call-update) | async-done | bytes 524304 | tf_op jit(solution)/shard_map/reduce_scatter | solution.py:89
  (184 shorter events, 155.6 us)
Async XLA Ops:
  7.2 22.4 %all-gather.5.cloned.1.call-start = ((), (), s32[]{:S(2)}) async-start(), calls=%async_computation.4 | async-start | bytes 1310720 | tf_op jit(solution)/shard_map/all_gather | solution.py:86
  9.0 201.8 %reduce-scatter.5.cloned.1.call-start = ((), (), s32[]{:S(2)}) async-start(), calls=%async_computation.5 | async-start | bytes 4718592 | tf_op jit(solution)/shard_map/reduce_scatter | solution.py:100
  29.6 2.4 copy-start.2
  29.6 2.4 copy-start.18
  29.6 2.4 copy-start.19
  123.7 87.1 %copy-start.9 = (f32[512,256]{1,0:T(8,128)S(1)}, f32[512,256]{1,0:T(8,128)}, u32[]{:S(2)}) copy-start(f32[512,256]{1,0:T(8,128)} %param.33) | copy-start | bytes 1572868
  123.7 87.1 %copy-start.11 = (f32[512,256]{1,0:T(8,128)S(1)}, f32[512,256]{1,0:T(8,128)}, u32[]{:S(2)}) copy-start(f32[512,256]{1,0:T(8,128)} %param.32) | copy-start | bytes 1572868
  123.7 87.1 %copy-start.13 = (f32[512,256]{1,0:T(8,128)S(1)}, f32[512,256]{1,0:T(8,128)}, u32[]{:S(2)}) copy-start(f32[512,256]{1,0:T(8,128)} %param.30) | copy-start | bytes 1572868
  123.7 87.1 %copy-start.17 = (f32[512,256]{1,0:T(8,128)S(1)}, f32[512,256]{1,0:T(8,128)}, u32[]{:S(2)}) copy-start(f32[512,256]{1,0:T(8,128)} %param.28) | copy-start | bytes 1572868
  123.7 87.1 %copy-start.21 = (f32[256]{0:T(256)S(1)}, f32[256]{0:T(256)}, u32[]{:S(2)}) copy-start(f32[256]{0:T(256)} %param.34) | copy-start | bytes 3076
  123.7 138.7 %all-gather.7.cloned.1.call-start = ((), (), s32[]{:S(2)}) async-start(), calls=%async_computation.6 | async-start | bytes 2359296 | tf_op jit(solution)/shard_map/all_gather | solution.py:103
  212.0 0.8 copy-start.6
  213.6 172.6 %reduce-scatter.7.cloned.1.call-start = ((), (), s32[]{:S(2)}) async-start(), calls=%async_computation.7 | async-start | bytes 2621440 | tf_op jit(solution)/shard_map/reduce_scatter | solution.py:89
  355.9 1.3 copy-start.1
  355.9 30.3 %copy-start.8 = (f32[512,256]{1,0:T(8,128)S(1)}, f32[512,256]{1,0:T(8,128)}, u32[]{:S(2)}) copy-start(f32[512,256]{1,0:T(8,128)} %param.29) | copy-start | bytes 1572868
  355.9 30.3 %copy-start.15 = (f32[512,256]{1,0:T(8,128)S(1)}, f32[512,256]{1,0:T(8,128)}, u32[]{:S(2)}) copy-start(f32[512,256]{1,0:T(8,128)} %param.31) | copy-start | bytes 1572868
  355.9 30.2 %copy-start.20 = (f32[256]{0:T(256)S(1)}, f32[256]{0:T(256)}, u32[]{:S(2)}) copy-start(f32[256]{0:T(256)} %param.35) | copy-start | bytes 3076
  357.2 48.6 %all-gather.9.cloned.1.call-start = ((), (), s32[]{:S(2)}) async-start(), calls=%async_computation.8 | async-start | bytes 1310720 | tf_op jit(solution)/shard_map/all_gather | solution.py:86
  387.4 0.8 copy-start.4
  388.9 198.2 %reduce-scatter.9.cloned.1.call-start = ((), (), s32[]{:S(2)}) async-start(), calls=%async_computation.9 | async-start | bytes 4718592 | tf_op jit(solution)/shard_map/reduce_scatter | solution.py:100
  405.8 2.4 copy-start.3
  500.1 87.0 %copy-start.7 = (f32[512,256]{1,0:T(8,128)S(1)}, f32[512,256]{1,0:T(8,128)}, u32[]{:S(2)}) copy-start(f32[512,256]{1,0:T(8,128)} %copy-done.6) | copy-start | bytes 1572868
  500.1 87.0 %copy-start.10 = (f32[512,256]{1,0:T(8,128)S(1)}, f32[512,256]{1,0:T(8,128)}, u32[]{:S(2)}) copy-start(f32[512,256]{1,0:T(8,128)} %param.33) | copy-start | bytes 1572868
  500.1 87.0 %copy-start.12 = (f32[512,256]{1,0:T(8,128)S(1)}, f32[512,256]{1,0:T(8,128)}, u32[]{:S(2)}) copy-start(f32[512,256]{1,0:T(8,128)} %param.32) | copy-start | bytes 1572868
  500.1 87.0 %copy-start.14 = (f32[512,256]{1,0:T(8,128)S(1)}, f32[512,256]{1,0:T(8,128)}, u32[]{:S(2)}) copy-start(f32[512,256]{1,0:T(8,128)} %param.30) | copy-start | bytes 1572868
  500.1 138.4 %all-gather.11.cloned.1.call-start = ((), (), s32[]{:S(2)}) async-start(), calls=%async_computation.10 | async-start | bytes 2359296 | tf_op jit(solution)/shard_map/all_gather | solution.py:103
  589.2 173.5 %reduce-scatter.11.cloned.1.call-start = ((), (), s32[]{:S(2)}) async-start(), calls=%async_computation.11 | async-start | bytes 2621440 | tf_op jit(solution)/shard_map/reduce_scatter | solution.py:89
  732.4 1.3 copy-start
  732.4 30.3 %copy-start.5 = (f32[512,256]{1,0:T(8,128)S(1)}, f32[512,256]{1,0:T(8,128)}, u32[]{:S(2)}) copy-start(f32[512,256]{1,0:T(8,128)} %copy-done.4) | copy-start | bytes 1572868
  732.4 30.3 %copy-start.16 = (f32[512,256]{1,0:T(8,128)S(1)}, f32[512,256]{1,0:T(8,128)}, u32[]{:S(2)}) copy-start(f32[512,256]{1,0:T(8,128)} %param.31) | copy-start | bytes 1572868
Sparse Core Ops, SparseCore 0:
  10.1 19.4 all-gather.4
  123.9 86.8 reduce-scatter.4
  213.7 48.7 all-gather.6
  357.4 28.7 reduce-scatter.6
  389.0 16.7 all-gather.8
  500.3 86.7 reduce-scatter.8
  589.8 48.7 all-gather.10
  733.9 28.7 reduce-scatter.10
